TPU v7x, 256 devices: a whole 4x4x8 slice. The times are simulated.
256 devices in a mesh: node: 64 (over z, x, core), freq: 4 (over y).
Axes of the slice: x: 4, y: 4, z: 8, core: 2. Of those that a mesh axis runs over, the one named last changes fastest.
Arguments:
- action_old: float32 [36, 36, 32768], P('freq', None, 'node'), may hold values from 0.05 to 2
- source: float32 [36, 36, 32768], P('freq', None, 'node'), may hold values from -4 to 4
- time_weight: float32 [32768], P('node'), may hold values from 0.5 to 4
- group_speed: float32 [36], P('freq'), may hold values from 0.3 to 3
- normals: float32 [2, 8, 32768], P(None, None, 'node'), may hold values from -3 to 3
- refract: float32 [32768], P('node'), may hold values from -4 to 4
- freq_shift: float32 [32768], P('node'), may hold values from -4 to 4
- nbr_list: int32 [64, 6], P('node'), may hold values from -1 to 63, as said below
- send_nodes: int32 [64, 6, 32], P('node'), may hold values from 0 to 511, as said below
- adjacency: int32 [8, 32768], P(None, 'node'), may hold values from 0 to 703, as said below
Outputs:
- action_new: float32 [36, 36, 32768], P('freq', None, 'node')
Inputs may be any that keep to these rules, and one draw needn't show every extreme that they name: `nbr_list`: slot entries of subdomain p are distinct subdomains (p + o) or (p - o) modulo the number of subdomains, 1 <= o <= 3, or -1 for an empty slot; p + 1 and p - 1 are always listed; if p lists q then q lists p. `send_nodes`: local node indices of the sending subdomain. `adjacency`: entries as in the first step; an entry at or above 512 never names an empty slot.
All inputs are finite; a program needn't handle non-finite values.
Results may differ from a plain program's by a relative error of at most 0.000088.
Values sent between devices are 32-bit elements; how exact they have to be, the bound alone decides.
A program may use at most 128 MiB of HBM per device.

v0:
```python
import functools
import math

import jax
import jax.numpy as jnp
import numpy as np
from jax import lax
from jax.experimental import pallas as pl
from jax.experimental.pallas import tpu as pltpu
from jax.sharding import PartitionSpec as P

REACH = 3
ITERS = 3
MESH = pl.DeviceIdType.MESH
F32 = jnp.float32
BF16 = jnp.bfloat16
GROUPS = ((0, 4, 8), (1, 2, 3), (5, 6, 7))
OFFSETS = tuple(sign * reach for reach in range(1, REACH + 1) for sign in (1, -1))


def split(value):
    high = value.astype(BF16)
    low = (value - high.astype(F32)).astype(BF16)
    return high, low


def kernel(
    node_count,
    freq_count,
    old_hbm,
    source_hbm,
    weight_ref,
    refract_ref,
    shift_ref,
    speed_ref,
    normals_ref,
    nbr_ref,
    send_ref,
    adjacency_ref,
    trig_ref,
    out_hbm,
    old_in,
    source_in,
    out_vmem,
    spectra,
    steady,
    inverse,
    edge_weight,
    turn,
    pick_local,
    pick_halo,
    select,
    parts,
    parcel_out,
    parcel_in,
    band_in,
    load_sem,
    store_sem,
    send_sem,
    recv_sem,
    band_send_sem,
    band_recv_sem,
):
    bands, angles, local = old_in.shape
    rows = spectra.shape[2]
    degree = adjacency_ref.shape[0]
    slots, _, width = send_ref.shape
    halo = slots * width
    per_group = len(GROUPS[0])
    half = per_group * rows
    me = lax.axis_index("node")
    band_me = lax.axis_index("freq")

    def node_at(offset):
        return lax.rem(me + offset + node_count, node_count)

    def band_at(offset):
        return lax.rem(band_me + offset + freq_count, freq_count)

    loads = [
        pltpu.make_async_copy(old_hbm, old_in, load_sem.at[0]),
        pltpu.make_async_copy(source_hbm, source_in, load_sem.at[1]),
    ]
    for load in loads:
        load.start()
    barrier = pltpu.get_barrier_semaphore()
    for offset in OFFSETS:
        pl.semaphore_signal(
            barrier, inc=1, device_id={"node": node_at(offset)}, device_id_type=MESH
        )
    for offset in (1, -1):
        pl.semaphore_signal(
            barrier, inc=1, device_id={"freq": band_at(offset)}, device_id_type=MESH
        )

    def parcel(step, group, j):
        piece = pl.ds(j * width, width)
        return pltpu.make_async_remote_copy(
            src_ref=parcel_out.at[step, group, piece],
            dst_ref=parcel_in.at[step, group, piece],
            send_sem=send_sem.at[step, group, j],
            recv_sem=recv_sem.at[step, group, j],
            device_id={"node": node_at(OFFSETS[j])},
            device_id_type=MESH,
        )

    def band_copy(step, side):
        return pltpu.make_async_remote_copy(
            src_ref=spectra.at[step, (bands - 1, 0)[side]],
            dst_ref=band_in.at[step, side],
            send_sem=band_send_sem.at[step, side],
            recv_sem=band_recv_sem.at[step, side],
            device_id={"freq": band_at((1, -1)[side])},
            device_id_type=MESH,
        )

    def send_group(step, group):
        if group == 0:
            for side in range(2):
                band_copy(step, side).start()
        picked = jnp.dot(parts[group], select[...], preferred_element_type=F32)
        picked = picked[:half] + picked[half:]
        picked = jnp.concatenate([picked, jnp.zeros((128 - half, picked.shape[1]), F32)], axis=0)
        parcel_out[step, group] = picked.T[:halo]
        for j in range(len(OFFSETS)):
            parcel(step, group, j).start()

    def set_parts(group, i, value):
        high, low = split(value)
        parts[group, pl.ds(i * rows, rows)] = high
        parts[group, pl.ds(half + i * rows, rows)] = low

    chosen = []
    for offset in OFFSETS:
        target = node_at(offset)
        row = jnp.zeros((1, width), jnp.int32)
        for s in range(slots):
            row = row + jnp.where(nbr_ref[0, s] == target, send_ref[s], 0)
        chosen.append(row)
    fill = jnp.full((1, select.shape[1] - halo), -1, jnp.int32)
    chosen = jnp.concatenate(chosen + [fill], axis=1)
    node_ids = lax.broadcasted_iota(jnp.int32, select.shape, 0)
    select[...] = jnp.where(node_ids == chosen, 1.0, 0.0).astype(BF16)

    loads[0].wait()
    for group, members in enumerate(GROUPS):
        for i, f in enumerate(members):
            value = old_in[f]
            first, last = value[0:1], value[angles - 1 : angles]
            value = jnp.concatenate([value, first, first, last, last], axis=0)
            spectra[0, f] = value
            set_parts(group, i, value)
    pl.semaphore_wait(barrier, len(OFFSETS) + 2)
    for group in range(len(GROUPS)):
        send_group(0, group)

    adjacency = adjacency_ref[...]
    own = lax.broadcasted_iota(jnp.int32, adjacency.shape, 1)
    used = adjacency != own
    relative = adjacency - local
    slot_of = relative // width
    moved = jnp.zeros_like(adjacency)
    for s in range(slots):
        place = jnp.int32(0)
        for j, offset in enumerate(OFFSETS):
            place = place + jnp.where(nbr_ref[0, s] == node_at(-offset), (j - s) * width, 0)
        moved = moved + jnp.where(slot_of == s, place, 0)
    in_halo = jnp.where(adjacency >= local, relative + moved, -1)
    local_ids = lax.broadcasted_iota(jnp.int32, (local, local), 0)
    halo_ids = lax.broadcasted_iota(jnp.int32, (halo, local), 0)
    for k in range(degree):
        pick_local[k] = jnp.where(local_ids == adjacency[k : k + 1], 1.0, 0.0).astype(BF16)
        pick_halo[k] = jnp.where(halo_ids == in_halo[k : k + 1], 1.0, 0.0).astype(BF16)

    cosine = jnp.broadcast_to(trig_ref[:, 0:1], (rows, local))
    sine = jnp.broadcast_to(trig_ref[:, 1:2], (rows, local))
    across = jnp.where(used, normals_ref[0], 0.0)
    along = jnp.where(used, normals_ref[1], 0.0)
    outward = jnp.zeros((rows, local), F32)
    for k in range(degree):
        flux = cosine * across[k : k + 1] + sine * along[k : k + 1]
        outward = outward + jnp.maximum(flux, 0.0)
        edge_weight[k] = jnp.maximum(-flux, 0.0)
    time_weight = weight_ref[...]
    freq_shift = shift_ref[...]
    turning = refract_ref[...] * cosine
    turn[0] = jnp.maximum(turning, 0.0)
    turn[1] = jnp.maximum(-turning, 0.0)
    fixed = time_weight + jnp.abs(turning) + jnp.abs(freq_shift)
    loads[1].wait()
    pad = jnp.zeros((rows - angles, local), F32)
    for f in range(bands):
        inverse[f] = 1.0 / (fixed + speed_ref[0, f] * outward)
        steady[f] = time_weight * spectra[0, f] + jnp.concatenate([source_in[f], pad], axis=0)

    sublane = lax.broadcasted_iota(jnp.int32, (8, local), 0)

    def step_of(step, carry):
        rising = jnp.maximum(freq_shift, 0.0)
        falling = jnp.maximum(-freq_shift, 0.0)
        for group, members in enumerate(GROUPS):
            sums = [jnp.zeros((rows, local), F32) for _ in members]

            def add(sums, left, right_ref):
                for k in range(degree):
                    got = jnp.dot(left, right_ref[k], preferred_element_type=F32)
                    got = got[:half] + got[half:]
                    weight = edge_weight[k]
                    sums = [
                        part + weight * got[i * rows : (i + 1) * rows]
                        for i, part in enumerate(sums)
                    ]
                return sums

            sums = add(sums, parts[group], pick_local)
            for j in range(len(OFFSETS)):
                parcel(step, group, j).wait_recv()
            arrived = parcel_in[step, group].T[:half]
            sums = add(sums, jnp.concatenate(split(arrived), axis=0), pick_halo)
            if group == 0:
                for side in range(2):
                    band_copy(step, side).wait_recv()
            for i, f in enumerate(members):
                value = spectra[step, f]
                inflow = turn[0] * pltpu.roll(value, 1, 0) + turn[1] * pltpu.roll(value, rows - 1, 0)
                if f > 0:
                    below = spectra[step, f - 1]
                else:
                    below = jnp.where(band_me > 0, band_in[step, 0], 0.0)
                if f < bands - 1:
                    above = spectra[step, f + 1]
                else:
                    above = jnp.where(band_me < freq_count - 1, band_in[step, 1], 0.0)
                inflow = inflow + rising * below + falling * above
                value = (steady[f] + inflow + speed_ref[0, f] * sums[i]) * inverse[f]

                @pl.when(step == ITERS - 1)
                def _():
                    out_vmem[f] = value[:angles]
                    pltpu.make_async_copy(out_vmem.at[f], out_hbm.at[f], store_sem.at[f]).start()

                @pl.when(step < ITERS - 1)
                def _():
                    first, last = value[:8], value[rows - 8 :]
                    end = jnp.where(sublane == 7, pltpu.roll(last, 4, 0), last)
                    end = jnp.where(sublane == 4, pltpu.roll(first, 4, 0), end)
                    whole = jnp.concatenate([value[: rows - 8], end], axis=0)
                    spectra[step + 1, f] = whole
                    set_parts(group, i, whole)

            @pl.when(step < ITERS - 1)
            def _():
                send_group(step + 1, group)

        return carry

    lax.fori_loop(0, ITERS, step_of, 0)

    for step in range(ITERS):
        for group in range(len(GROUPS)):
            for j in range(len(OFFSETS)):
                parcel(step, group, j).wait_send()
        for side in range(2):
            band_copy(step, side).wait_send()
    for f in range(bands):
        pltpu.make_async_copy(out_vmem.at[f], out_hbm.at[f], store_sem.at[f]).wait()


def body(
    node_count,
    freq_count,
    action_old,
    source,
    time_weight,
    group_speed,
    normals,
    refract,
    freq_shift,
    nbr_list,
    send_nodes,
    adjacency,
):
    bands, angles, local = action_old.shape
    degree = adjacency.shape[0]
    slots, width = send_nodes.shape[1:]
    rows = -(-(angles + 2) // 8) * 8
    groups = len(GROUPS)
    half = len(GROUPS[0]) * rows
    halo = slots * width
    turns = np.concatenate([np.arange(angles), [0, 0, angles - 1, angles - 1]])
    theta = 2.0 * math.pi * turns / angles
    trig = np.zeros((rows, 128), np.float32)
    trig[:, 0] = np.cos(theta)
    trig[:, 1] = np.sin(theta)
    vmem = pl.BlockSpec(memory_space=pltpu.VMEM)
    smem = pl.BlockSpec(memory_space=pltpu.SMEM)
    anywhere = pl.BlockSpec(memory_space=pl.ANY)
    dma = pltpu.SemaphoreType.DMA
    return pl.pallas_call(
        functools.partial(kernel, node_count, freq_count),
        out_shape=jax.ShapeDtypeStruct(action_old.shape, F32),
        in_specs=[anywhere, anywhere, vmem, vmem, vmem, smem, vmem, smem, vmem, vmem, vmem],
        out_specs=anywhere,
        scratch_shapes=[
            pltpu.VMEM((bands, angles, local), F32),
            pltpu.VMEM((bands, angles, local), F32),
            pltpu.VMEM((bands, angles, local), F32),
            pltpu.VMEM((ITERS, bands, rows, local), F32),
            pltpu.VMEM((bands, rows, local), F32),
            pltpu.VMEM((bands, rows, local), F32),
            pltpu.VMEM((degree, rows, local), F32),
            pltpu.VMEM((2, rows, local), F32),
            pltpu.VMEM((degree, local, local), BF16),
            pltpu.VMEM((degree, halo, local), BF16),
            pltpu.VMEM((local, 256), BF16),
            pltpu.VMEM((groups, 2 * half, local), BF16),
            pltpu.VMEM((ITERS, groups, halo, 128), F32),
            pltpu.VMEM((ITERS, groups, halo, 128), F32),
            pltpu.VMEM((ITERS, 2, rows, local), F32),
            dma((2,)),
            dma((bands,)),
            dma((ITERS, groups, slots)),
            dma((ITERS, groups, slots)),
            dma((ITERS, 2)),
            dma((ITERS, 2)),
        ],
        compiler_params=pltpu.CompilerParams(
            collective_id=0, has_side_effects=True, vmem_limit_bytes=62 * 1024 * 1024
        ),
    )(
        action_old,
        source,
        time_weight[None, :],
        refract[None, :],
        freq_shift[None, :],
        group_speed[None, :],
        normals,
        nbr_list,
        send_nodes.reshape(slots, 1, width),
        adjacency,
        jnp.asarray(trig),
    )


def solution(mesh):
    in_specs = (
        P("freq", None, "node"),
        P("freq", None, "node"),
        P("node"),
        P("freq"),
        P(None, None, "node"),
        P("node"),
        P("node"),
        P("node", None),
        P("node", None, None),
        P(None, "node"),
    )
    return jax.shard_map(
        functools.partial(body, mesh.shape["node"], mesh.shape["freq"]),
        mesh=mesh,
        in_specs=in_specs,
        out_specs=P("freq", None, "node"),
        check_vma=False,
    )
```

profile of v0, /device:TPU:1, one launch (start us, length us, event | category | flops | bytes accessed | tf_op | source)
XLA Modules:
  0.0 39.0 jit_solution(7141936224142875002)
XLA Ops:
  0.0 37.0 %shard_map.109 = f32[9,36,512]{2,1,0:T(8,128)} custom-call(f32[9,36,512]{2,1,0:T(8,128)} %old_hbm.1, f32[9,36,512]{2,1,0:T(8,128)} %source_hbm.1, f32[1,512]{1,0:T(1,128)} %bitcast.6, f32[1,512]{1,0:T(1,128)} %bitcast.7, f32[1,512]{1,0:T(1,128)} %bitcast.8, f32[1,9]{1,0:T(1,128)} %bitcast.9, f32[2,8,512]{2,1,0:T(8,128)} %normals_ref.1, s32[1,6]{1,0:T(1,128)} %nbr_ref.1, ...), custom_call_target="tpu_custom_call" | custom-call | tf_op jit(solution)/shard_map/pallas_call | solution.py:299
  37.0 2.0 %copy.13 = f32[9,36,512]{2,1,0:T(8,128)} copy(f32[9,36,512]{2,1,0:T(8,128)} %shard_map.109) | data formatting | bytes 1327104
where the time goes:
time: 39.2 us; the launch traced here: 39 us
  Pallas kernels  37 us (94%)
  local copies, waits for them, and re-layouts  2.03 us (5%)
    pallas_call x1, Pallas kernels, body(): pl.pallas_call(functools.partial(kernel, node_count, freq_count), out_sha...  37 us
    unnamed x1, local copies, waits for them, and re-layouts  2.03 us

commit v1 on v0

v1 whole, which is shorter than its diff:
```python
import functools
import math

import jax
import jax.numpy as jnp
import numpy as np
from jax import lax
from jax.experimental import pallas as pl
from jax.experimental.pallas import tpu as pltpu
from jax.sharding import PartitionSpec as P

REACH = 3
ITERS = 3
MESH = pl.DeviceIdType.MESH
F32 = jnp.float32
BF16 = jnp.bfloat16
OFFSETS = tuple(sign * reach for reach in range(1, REACH + 1) for sign in (1, -1))
STRIDE = 3
ORDER = (0, 2, 1)
TILE = 256
AHEAD = 4
VMEM_LIMIT = 62 * 1024 * 1024


def split(value):
    high = value.astype(BF16)
    low = (value - high.astype(F32)).astype(BF16)
    return high, low


class Units:
    def __init__(self, jobs):
        self.jobs = jobs
        self.at = [0, 0]
        for unit in range(2):
            self.stage(unit, 0)

    def stage(self, unit, index):
        if index < len(self.jobs[unit]):
            matrix = self.jobs[unit][index][0]()
            pltpu.matmul_push_rhs(matrix, staging_register=index % 2, mxu_index=unit)

    def run(self, count):
        for _ in range(count):
            for unit in range(2):
                index = self.at[unit]
                self.stage(unit, index + 1)
                _, total, high, low = self.jobs[unit][index]
                pltpu.matmul_acc_lhs(total, high(), load_staged_rhs=index % 2)
                pltpu.matmul_acc_lhs(total, low())
                self.at[unit] = index + 1


def kernel(node_count, freq_count, *refs):
    (old_hbm,) = refs[:1]
    speed_ref = refs[5]
    degree = refs[9].shape[0]
    block = refs[14].shape[2]
    count = degree + 1
    specs = [pltpu.ACC(unit)((block, TILE), F32) for unit in range(2) for _ in range(count)]

    def scoped(*totals):
        run(node_count, freq_count, (totals[:count], totals[count:]), *refs)

    pl.run_scoped(scoped, *specs)


def run(
    node_count,
    freq_count,
    totals,
    old_hbm,
    source_hbm,
    weight_ref,
    refract_ref,
    shift_ref,
    speed_ref,
    normals_ref,
    nbr_ref,
    send_ref,
    adjacency_ref,
    trig_ref,
    out_ref,
    old_in,
    source_in,
    spectra,
    base,
    inverse,
    speed_inverse,
    edge_weight,
    turn,
    pick_local,
    pick_halo,
    select,
    parts,
    halo_parts,
    sums,
    parcel_out,
    parcel_in,
    band_in,
    load_sem,
    send_sem,
    recv_sem,
    band_send_sem,
    band_recv_sem,
):
    bands, angles, local = old_in.shape
    groups, block = spectra.shape[1:3]
    edge = band_in.shape[2]
    degree = adjacency_ref.shape[0]
    slots, _, width = send_ref.shape
    halo = slots * width
    members = bands // groups
    me = lax.axis_index("node")
    band_me = lax.axis_index("freq")

    def node_at(offset):
        return lax.rem(me + offset + node_count, node_count)

    def band_at(offset):
        return lax.rem(band_me + offset + freq_count, freq_count)

    loads = [
        pltpu.make_async_copy(old_hbm, old_in, load_sem.at[0]),
        pltpu.make_async_copy(source_hbm, source_in, load_sem.at[1]),
    ]
    for load in loads:
        load.start()
    barrier = pltpu.get_barrier_semaphore()
    for offset in OFFSETS:
        pl.semaphore_signal(
            barrier, inc=1, device_id={"node": node_at(offset)}, device_id_type=MESH
        )
    for offset in (1, -1):
        pl.semaphore_signal(
            barrier, inc=1, device_id={"freq": band_at(offset)}, device_id_type=MESH
        )

    def parcel(step, group, j):
        piece = pl.ds(j * width, width)
        return pltpu.make_async_remote_copy(
            src_ref=parcel_out.at[step, group, piece],
            dst_ref=parcel_in.at[step, group, piece],
            send_sem=send_sem.at[step, group, j],
            recv_sem=recv_sem.at[step, group, j],
            device_id={"node": node_at(OFFSETS[j])},
            device_id_type=MESH,
        )

    def band_copy(step, side):
        row = (block - edge, 0)[side]
        return pltpu.make_async_remote_copy(
            src_ref=spectra.at[step, (groups - 1, 0)[side], pl.ds(row, edge)],
            dst_ref=band_in.at[step, side],
            send_sem=band_send_sem.at[step, side],
            recv_sem=band_recv_sem.at[step, side],
            device_id={"freq": band_at((1, -1)[side])},
            device_id_type=MESH,
        )

    def cut(k):
        return pl.ds(k * TILE, TILE)

    def lhs(group, part, k):
        return lambda: parts[group, part, :, cut(k)]

    def local_jobs(group, entries):
        return [
            [
                (
                    lambda k=k, m=m, unit=unit: pick_local[k, cut(m), cut(unit)],
                    totals[unit][k],
                    lhs(group, 0, m),
                    lhs(group, 1, m),
                )
                for k in entries
                for m in range(local // TILE)
            ]
            for unit in range(2)
        ]

    def halo_jobs(turn_index):
        slot = turn_index % 2
        return [
            [
                (
                    lambda k=k, unit=unit: pick_halo[k, :, cut(unit)],
                    totals[unit][k],
                    lambda: halo_parts[slot, 0],
                    lambda: halo_parts[slot, 1],
                )
                for k in range(degree)
            ]
            for unit in range(2)
        ]

    def select_jobs(group):
        return [
            [
                (
                    lambda unit=unit: select[cut(unit), :],
                    totals[unit][degree],
                    lhs(group, 0, unit),
                    lhs(group, 1, unit),
                )
            ]
            for unit in range(2)
        ]

    def join(*lists):
        return [[job for jobs in lists for job in jobs[unit]] for unit in range(2)]

    def send_group(step, group):
        picked = pltpu.matmul_pop(totals[0][degree]) + pltpu.matmul_pop(totals[1][degree])
        picked = jnp.concatenate([picked, jnp.zeros((128 - block, TILE), F32)], axis=0)
        parcel_out[step, group] = picked.T[:halo]
        for j in range(len(OFFSETS)):
            parcel(step, group, j).start()

    for unit in range(2):
        for total in totals[unit]:
            pltpu.matmul_pop(total)

    chosen = []
    for offset in OFFSETS:
        target = node_at(offset)
        row = jnp.zeros((1, width), jnp.int32)
        for s in range(slots):
            row = row + jnp.where(nbr_ref[0, s] == target, send_ref[s], 0)
        chosen.append(row)
    fill = jnp.full((1, select.shape[1] - halo), -1, jnp.int32)
    chosen = jnp.concatenate(chosen + [fill], axis=1)
    node_ids = lax.broadcasted_iota(jnp.int32, select.shape, 0)
    select[...] = jnp.where(node_ids == chosen, 1.0, 0.0).astype(BF16)

    def pack(ref, group):
        rows = [ref[group + i * STRIDE] for i in range(members)]
        fill = jnp.zeros((block - members * angles, local), F32)
        return jnp.concatenate(rows + [fill], axis=0)

    loads[0].wait()
    for group in ORDER:
        value = pack(old_in, group)
        spectra[0, group] = value
        parts[group, 0], parts[group, 1] = split(value)
    units = Units(join(*[select_jobs(group) for group in ORDER]))
    pl.semaphore_wait(barrier, len(OFFSETS) + 2)
    for side in range(2):
        band_copy(0, side).start()
    for group in ORDER:
        units.run(1)
        send_group(0, group)

    adjacency = adjacency_ref[...]
    own = lax.broadcasted_iota(jnp.int32, adjacency.shape, 1)
    used = adjacency != own
    relative = adjacency - local
    slot_of = relative // width
    moved = jnp.zeros_like(adjacency)
    for s in range(slots):
        place = jnp.int32(0)
        for j, offset in enumerate(OFFSETS):
            place = place + jnp.where(nbr_ref[0, s] == node_at(-offset), (j - s) * width, 0)
        moved = moved + jnp.where(slot_of == s, place, 0)
    in_halo = jnp.where(adjacency >= local, relative + moved, -1)
    chunk = 32
    first_ids = lax.broadcasted_iota(jnp.int32, (chunk, local), 0)

    def fill_from(out, target):
        def fill(c, carry):
            at = pl.multiple_of(c * chunk, chunk)
            ids = first_ids + at
            for k in range(degree):
                hit = jnp.where(ids == target[k : k + 1], 1.0, 0.0)
                out[k, pl.ds(at, chunk), :] = hit.astype(BF16)
            return carry

        lax.fori_loop(0, out.shape[1] // chunk, fill, 0)

    fill_from(pick_local, adjacency)
    fill_from(pick_halo, in_halo)

    period = 2 * angles
    cosine = jnp.broadcast_to(trig_ref[:, 0:1], (period, local))
    sine = jnp.broadcast_to(trig_ref[:, 1:2], (period, local))
    across = jnp.where(used, normals_ref[0], 0.0)
    along = jnp.where(used, normals_ref[1], 0.0)
    outward = jnp.zeros((period, local), F32)
    for k in range(degree):
        flux = cosine * across[k : k + 1] + sine * along[k : k + 1]
        outward = outward + jnp.maximum(flux, 0.0)
        inward = jnp.maximum(-flux, 0.0)
        edge_weight[k, pl.ds(0, period)] = inward
        edge_weight[k, pl.ds(period, block - period)] = inward[: block - period]
    time_weight = weight_ref[...]
    freq_shift = shift_ref[...]
    turning = refract_ref[...] * cosine
    for i, one in enumerate((turning, -turning)):
        one = jnp.maximum(one, 0.0)
        turn[i, pl.ds(0, period)] = one
        turn[i, pl.ds(period, block - period)] = one[: block - period]
    fixed = time_weight + jnp.abs(turning) + jnp.abs(freq_shift)
    outward = jnp.concatenate([outward, outward[: block - period]], axis=0)
    fixed = jnp.concatenate([fixed, fixed[: block - period]], axis=0)
    loads[1].wait()
    row_ids = lax.broadcasted_iota(jnp.int32, (block, local), 0)
    for group in ORDER:
        speed = jnp.full((block, local), speed_ref[0, group], F32)
        for i in range(1, members):
            speed = jnp.where(row_ids >= i * angles, speed_ref[0, group + i * STRIDE], speed)
        one = 1.0 / (fixed + speed * outward)
        inverse[group] = one
        speed_inverse[group] = speed * one
        base[group] = (time_weight * spectra[0, group] + pack(source_in, group)) * one

    rising = jnp.maximum(freq_shift, 0.0)
    falling = jnp.maximum(-freq_shift, 0.0)
    half_rows = lax.broadcasted_iota(jnp.int32, (block, TILE), 0)
    is_first = functools.reduce(jnp.logical_or, [half_rows == i * angles for i in range(members)])
    is_last = functools.reduce(
        jnp.logical_or, [half_rows == i * angles + angles - 1 for i in range(members)]
    )
    tail = jnp.zeros((block - members * angles, TILE), F32)

    def update(step, group, unit):
        columns = cut(unit)
        total = jnp.zeros((block, TILE), F32)
        for k in range(degree):
            total = total + edge_weight[k, :, columns] * pltpu.matmul_pop(totals[unit][k])
        sums[:, columns] = total

    def finish(step, group, unit):
        columns = cut(unit)
        value = spectra[step, group, :, columns]
        before = jnp.where(
            is_first, pltpu.roll(value, block - angles + 1, 0), pltpu.roll(value, 1, 0)
        )
        after = jnp.where(
            is_last, pltpu.roll(value, angles - 1, 0), pltpu.roll(value, block - 1, 0)
        )
        if group > 0:
            below = spectra[step, group - 1, :, columns]
        else:
            rim = band_in[step, 0, :, columns]
            rim = jnp.where(band_me > 0, rim[:angles], 0.0)
            moved = spectra[step, groups - 1, :, columns]
            below = jnp.concatenate([rim, moved[: (members - 1) * angles], tail], axis=0)
        if group < groups - 1:
            above = spectra[step, group + 1, :, columns]
        else:
            rim = band_in[step, 1, :, columns]
            rim = jnp.where(band_me < freq_count - 1, rim[:angles], 0.0)
            moved = spectra[step, 0, :, columns]
            above = jnp.concatenate([moved[angles : members * angles], rim, tail], axis=0)
        inflow = turn[0, :, columns] * before + turn[1, :, columns] * after
        inflow = inflow + rising[:, unit * TILE : (unit + 1) * TILE] * below
        inflow = inflow + falling[:, unit * TILE : (unit + 1) * TILE] * above
        value = base[group, :, columns] + inflow * inverse[group, :, columns]
        value = value + speed_inverse[group, :, columns] * sums[:, columns]
        if step == ITERS - 1:
            for i in range(members):
                out_ref[group + i * STRIDE, :, columns] = value[i * angles : (i + 1) * angles]
        else:
            spectra[step + 1, group, :, columns] = value
            high, low = split(value)
            parts[group, 0, :, columns] = high
            parts[group, 1, :, columns] = low

    turns = [(step, group) for step in range(ITERS) for group in ORDER]
    plan = [local_jobs(turns[0][1], range(AHEAD))]
    for index, (step, group) in enumerate(turns):
        plan.append(local_jobs(group, range(AHEAD, degree)))
        plan.append(halo_jobs(index))
        if index + 1 < len(turns):
            plan.append(local_jobs(turns[index + 1][1], range(AHEAD)))
        if step + 1 < ITERS:
            plan.append(select_jobs(group))
    units = Units(join(*plan))
    per_entry = local // TILE
    units.run(AHEAD * per_entry)
    for index, (step, group) in enumerate(turns):
        for j in range(len(OFFSETS)):
            parcel(step, group, j).wait_recv()
        if group == 0:
            band_copy(step, 0).wait_recv()
        if group == groups - 1:
            band_copy(step, 1).wait_recv()
        arrived = parcel_in[step, group].T[:block]
        arrived = jnp.concatenate([arrived, jnp.zeros((block, TILE - halo), F32)], axis=1)
        halo_parts[index % 2, 0], halo_parts[index % 2, 1] = split(arrived)
        units.run((degree - AHEAD) * per_entry)
        units.run(degree)
        for unit in range(2):
            update(step, group, unit)
        if index + 1 < len(turns):
            units.run(AHEAD * per_entry)
        for unit in range(2):
            finish(step, group, unit)
        if step + 1 < ITERS:
            if group == 0:
                band_copy(step + 1, 1).start()
            if group == groups - 1:
                band_copy(step + 1, 0).start()
            units.run(1)
            send_group(step + 1, group)

    for step in range(ITERS):
        for group in range(groups):
            for j in range(len(OFFSETS)):
                parcel(step, group, j).wait_send()
        for side in range(2):
            band_copy(step, side).wait_send()


def body(
    node_count,
    freq_count,
    action_old,
    source,
    time_weight,
    group_speed,
    normals,
    refract,
    freq_shift,
    nbr_list,
    send_nodes,
    adjacency,
):
    bands, angles, local = action_old.shape
    degree = adjacency.shape[0]
    slots, width = send_nodes.shape[1:]
    groups = STRIDE
    members = bands // groups
    block = -(-members * angles // 16) * 16
    edge = -(-angles // 8) * 8
    halo = slots * width
    theta = 2.0 * math.pi * (np.arange(2 * angles) % angles) / angles
    trig = np.zeros((2 * angles, 128), np.float32)
    trig[:, 0] = np.cos(theta)
    trig[:, 1] = np.sin(theta)
    vmem = pl.BlockSpec(memory_space=pltpu.VMEM)
    smem = pl.BlockSpec(memory_space=pltpu.SMEM)
    anywhere = pl.BlockSpec(memory_space=pl.ANY)
    dma = pltpu.SemaphoreType.DMA
    return pl.pallas_call(
        functools.partial(kernel, node_count, freq_count),
        out_shape=jax.ShapeDtypeStruct(action_old.shape, F32),
        in_specs=[anywhere, anywhere, vmem, vmem, vmem, smem, vmem, smem, vmem, vmem, vmem],
        out_specs=vmem,
        scratch_shapes=[
            pltpu.VMEM((bands, angles, local), F32),
            pltpu.VMEM((bands, angles, local), F32),
            pltpu.VMEM((ITERS, groups, block, local), F32),
            pltpu.VMEM((groups, block, local), F32),
            pltpu.VMEM((groups, block, local), F32),
            pltpu.VMEM((groups, block, local), F32),
            pltpu.VMEM((degree, block, local), F32),
            pltpu.VMEM((2, block, local), F32),
            pltpu.VMEM((degree, local, local), BF16),
            pltpu.VMEM((degree, TILE, local), BF16),
            pltpu.VMEM((local, TILE), BF16),
            pltpu.VMEM((groups, 2, block, local), BF16),
            pltpu.VMEM((2, 2, block, TILE), BF16),
            pltpu.VMEM((block, local), F32),
            pltpu.VMEM((ITERS, groups, halo, 128), F32),
            pltpu.VMEM((ITERS, groups, halo, 128), F32),
            pltpu.VMEM((ITERS, 2, edge, local), F32),
            dma((2,)),
            dma((ITERS, groups, slots)),
            dma((ITERS, groups, slots)),
            dma((ITERS, 2)),
            dma((ITERS, 2)),
        ],
        compiler_params=pltpu.CompilerParams(
            collective_id=0, has_side_effects=True, vmem_limit_bytes=VMEM_LIMIT
        ),
    )(
        action_old,
        source,
        time_weight[None, :],
        refract[None, :],
        freq_shift[None, :],
        group_speed[None, :],
        normals,
        nbr_list,
        send_nodes.reshape(slots, 1, width),
        adjacency,
        jnp.asarray(trig),
    )


def solution(mesh):
    in_specs = (
        P("freq", None, "node"),
        P("freq", None, "node"),
        P("node"),
        P("freq"),
        P(None, None, "node"),
        P("node"),
        P("node"),
        P("node", None),
        P("node", None, None),
        P(None, "node"),
    )
    return jax.shard_map(
        functools.partial(body, mesh.shape["node"], mesh.shape["freq"]),
        mesh=mesh,
        in_specs=in_specs,
        out_specs=P("freq", None, "node"),
        check_vma=False,
    )
```

time: 39.2 us -> 40.6 us (1.036)
  Pallas kernels: 37 us -> 38.3 us
    pallas_call x1, Pallas kernels: 37 us -> 38.3 us  [body(): pl.pallas_call(functools.partial(kernel, node_count, freq_count), out_sha...]
where the time goes in v1:
time: 40.6 us; the launch traced here: 40.4 us
  Pallas kernels  38.3 us (94%)
  local copies, waits for them, and re-layouts  2.03 us (5%)
    pallas_call x1, Pallas kernels, body(): pl.pallas_call(functools.partial(kernel, node_count, freq_count), out_sha...  38.3 us
    unnamed x1, local copies, waits for them, and re-layouts  2.03 us

profile of v1, /device:TPU:1, one launch (start us, length us, event | category | flops | bytes accessed | tf_op | source)
XLA Modules:
  0.0 40.4 jit_solution(6957220559238216358)
XLA Ops:
  0.0 38.3 %shard_map.109 = f32[9,36,512]{2,1,0:T(8,128)} custom-call(f32[9,36,512]{2,1,0:T(8,128)} %refs_0_.1, f32[9,36,512]{2,1,0:T(8,128)} %refs_1_.1, f32[1,512]{1,0:T(1,128)} %bitcast.6, f32[1,512]{1,0:T(1,128)} %bitcast.7, f32[1,512]{1,0:T(1,128)} %bitcast.8, f32[1,9]{1,0:T(1,128)} %bitcast.9, f32[2,8,512]{2,1,0:T(8,128)} %refs_6_.1, s32[1,6]{1,0:T(1,128)} %refs_7_.1, ...), custom_call_target="tpu_custom_call" | custom-call | tf_op jit(solution)/shard_map/pallas_call | solution.py:445
  38.3 2.0 %copy.13 = f32[9,36,512]{2,1,0:T(8,128)} copy(f32[9,36,512]{2,1,0:T(8,128)} %shard_map.109) | data formatting | bytes 1327104

commit v2 on v1

--- a/solution.py
+++ b/solution.py
@@ -18,8 +18,7 @@
 STRIDE = 3
 ORDER = (0, 2, 1)
 TILE = 256
-AHEAD = 4
-VMEM_LIMIT = 62 * 1024 * 1024
+VMEM_LIMIT = 66100000
 
 
 def split(value):
@@ -52,8 +51,6 @@
 
 
 def kernel(node_count, freq_count, *refs):
-    (old_hbm,) = refs[:1]
-    speed_ref = refs[5]
     degree = refs[9].shape[0]
     block = refs[14].shape[2]
     count = degree + 1
@@ -71,15 +68,15 @@
     totals,
     old_hbm,
     source_hbm,
-    weight_ref,
-    refract_ref,
-    shift_ref,
-    speed_ref,
-    normals_ref,
-    nbr_ref,
-    send_ref,
-    adjacency_ref,
-    trig_ref,
+    weight_hbm,
+    refract_hbm,
+    shift_hbm,
+    speed_hbm,
+    normals_hbm,
+    nbr_hbm,
+    send_hbm,
+    adjacency_hbm,
+    trig_hbm,
     out_ref,
     old_in,
     source_in,
@@ -94,11 +91,21 @@
     select,
     parts,
     halo_parts,
-    sums,
+    ready,
     parcel_out,
     parcel_in,
     band_in,
+    weight_ref,
+    refract_ref,
+    shift_ref,
+    speed_ref,
+    normals_ref,
+    nbr_ref,
+    send_ref,
+    adjacency_ref,
+    trig_ref,
     load_sem,
+    old_sem,
     send_sem,
     recv_sem,
     band_send_sem,
@@ -120,11 +127,28 @@
     def band_at(offset):
         return lax.rem(band_me + offset + freq_count, freq_count)
 
-    loads = [
-        pltpu.make_async_copy(old_hbm, old_in, load_sem.at[0]),
-        pltpu.make_async_copy(source_hbm, source_in, load_sem.at[1]),
-    ]
-    for load in loads:
+    def old_load(f):
+        return pltpu.make_async_copy(old_hbm.at[f], old_in.at[f], old_sem.at[f])
+
+    pairs = (
+        (nbr_hbm, nbr_ref),
+        (send_hbm, send_ref),
+        (adjacency_hbm, adjacency_ref),
+        (normals_hbm, normals_ref),
+        (trig_hbm, trig_ref),
+        (weight_hbm, weight_ref),
+        (refract_hbm, refract_ref),
+        (shift_hbm, shift_ref),
+        (speed_hbm, speed_ref),
+        (source_hbm, source_in),
+    )
+    loads = [pltpu.make_async_copy(*pair, load_sem.at[i]) for i, pair in enumerate(pairs)]
+    for load in loads[:2]:
+        load.start()
+    for group in ORDER:
+        for i in range(members):
+            old_load(group + i * STRIDE).start()
+    for load in loads[2:]:
         load.start()
     barrier = pltpu.get_barrier_semaphore()
     for offset in OFFSETS:
@@ -214,13 +238,21 @@
         picked = pltpu.matmul_pop(totals[0][degree]) + pltpu.matmul_pop(totals[1][degree])
         picked = jnp.concatenate([picked, jnp.zeros((128 - block, TILE), F32)], axis=0)
         parcel_out[step, group] = picked.T[:halo]
-        for j in range(len(OFFSETS)):
+        for j in reversed(range(len(OFFSETS))):
             parcel(step, group, j).start()
+
+    def send_bands(step, group):
+        if group == 0:
+            band_copy(step, 1).start()
+        if group == groups - 1:
+            band_copy(step, 0).start()
 
     for unit in range(2):
         for total in totals[unit]:
             pltpu.matmul_pop(total)
 
+    for load in loads[:2]:
+        load.wait()
     chosen = []
     for offset in OFFSETS:
         target = node_at(offset)
@@ -238,19 +270,20 @@
         fill = jnp.zeros((block - members * angles, local), F32)
         return jnp.concatenate(rows + [fill], axis=0)
 
-    loads[0].wait()
+    units = Units(join(*[select_jobs(group) for group in ORDER]))
+    pl.semaphore_wait(barrier, len(OFFSETS) + 2)
     for group in ORDER:
+        for i in range(members):
+            old_load(group + i * STRIDE).wait()
         value = pack(old_in, group)
         spectra[0, group] = value
         parts[group, 0], parts[group, 1] = split(value)
-    units = Units(join(*[select_jobs(group) for group in ORDER]))
-    pl.semaphore_wait(barrier, len(OFFSETS) + 2)
-    for side in range(2):
-        band_copy(0, side).start()
-    for group in ORDER:
         units.run(1)
         send_group(0, group)
-
+        send_bands(0, group)
+
+    for load in loads[2:-1]:
+        load.wait()
     adjacency = adjacency_ref[...]
     own = lax.broadcasted_iota(jnp.int32, adjacency.shape, 1)
     used = adjacency != own
@@ -302,7 +335,7 @@
     fixed = time_weight + jnp.abs(turning) + jnp.abs(freq_shift)
     outward = jnp.concatenate([outward, outward[: block - period]], axis=0)
     fixed = jnp.concatenate([fixed, fixed[: block - period]], axis=0)
-    loads[1].wait()
+    loads[-1].wait()
     row_ids = lax.broadcasted_iota(jnp.int32, (block, local), 0)
     for group in ORDER:
         speed = jnp.full((block, local), speed_ref[0, group], F32)
@@ -320,16 +353,18 @@
     is_last = functools.reduce(
         jnp.logical_or, [half_rows == i * angles + angles - 1 for i in range(members)]
     )
+    gap = jnp.zeros((angles, TILE), F32)
     tail = jnp.zeros((block - members * angles, TILE), F32)
-
-    def update(step, group, unit):
-        columns = cut(unit)
-        total = jnp.zeros((block, TILE), F32)
+    edge_rows = lax.broadcasted_iota(jnp.int32, (edge, TILE), 0)
+
+    def gathered(unit):
+        total = None
         for k in range(degree):
-            total = total + edge_weight[k, :, columns] * pltpu.matmul_pop(totals[unit][k])
-        sums[:, columns] = total
-
-    def finish(step, group, unit):
+            term = edge_weight[k, :, cut(unit)] * pltpu.matmul_pop(totals[unit][k])
+            total = term if total is None else total + term
+        return total
+
+    def prepare(step, group, unit):
         columns = cut(unit)
         value = spectra[step, group, :, columns]
         before = jnp.where(
@@ -341,22 +376,38 @@
         if group > 0:
             below = spectra[step, group - 1, :, columns]
         else:
-            rim = band_in[step, 0, :, columns]
-            rim = jnp.where(band_me > 0, rim[:angles], 0.0)
             moved = spectra[step, groups - 1, :, columns]
-            below = jnp.concatenate([rim, moved[: (members - 1) * angles], tail], axis=0)
+            below = jnp.concatenate([gap, moved[: (members - 1) * angles], tail], axis=0)
         if group < groups - 1:
             above = spectra[step, group + 1, :, columns]
         else:
-            rim = band_in[step, 1, :, columns]
-            rim = jnp.where(band_me < freq_count - 1, rim[:angles], 0.0)
             moved = spectra[step, 0, :, columns]
-            above = jnp.concatenate([moved[angles : members * angles], rim, tail], axis=0)
+            above = jnp.concatenate([moved[angles : members * angles], gap, tail], axis=0)
         inflow = turn[0, :, columns] * before + turn[1, :, columns] * after
         inflow = inflow + rising[:, unit * TILE : (unit + 1) * TILE] * below
         inflow = inflow + falling[:, unit * TILE : (unit + 1) * TILE] * above
         value = base[group, :, columns] + inflow * inverse[group, :, columns]
-        value = value + speed_inverse[group, :, columns] * sums[:, columns]
+        value = value + speed_inverse[group, :, columns] * ready[group, :, columns]
+        ready[group, :, columns] = value
+
+    def finish(step, group, unit):
+        columns = cut(unit)
+        value = ready[group, :, columns]
+        value = value + speed_inverse[group, :, columns] * gathered(unit)
+        if group == 0:
+            rim = band_in[step, 0, :, columns] * rising[:, unit * TILE : (unit + 1) * TILE]
+            rim = rim * inverse[group, pl.ds(0, edge), columns]
+            rim = jnp.where(jnp.logical_and(edge_rows < angles, band_me > 0), rim, 0.0)
+            value = jnp.concatenate([value[:edge] + rim, value[edge:]], axis=0)
+        if group == groups - 1:
+            rim = band_in[step, 1, :, columns] * falling[:, unit * TILE : (unit + 1) * TILE]
+            rim = rim * inverse[group, pl.ds(block - edge, edge), columns]
+            rim = jnp.where(
+                jnp.logical_and(edge_rows < angles, band_me < freq_count - 1), rim, 0.0
+            )
+            value = jnp.concatenate(
+                [value[: block - edge], value[block - edge :] + rim], axis=0
+            )
         if step == ITERS - 1:
             for i in range(members):
                 out_ref[group + i * STRIDE, :, columns] = value[i * angles : (i + 1) * angles]
@@ -366,43 +417,40 @@
             parts[group, 0, :, columns] = high
             parts[group, 1, :, columns] = low
 
-    turns = [(step, group) for step in range(ITERS) for group in ORDER]
-    plan = [local_jobs(turns[0][1], range(AHEAD))]
-    for index, (step, group) in enumerate(turns):
-        plan.append(local_jobs(group, range(AHEAD, degree)))
-        plan.append(halo_jobs(index))
-        if index + 1 < len(turns):
-            plan.append(local_jobs(turns[index + 1][1], range(AHEAD)))
-        if step + 1 < ITERS:
-            plan.append(select_jobs(group))
+    plan = []
+    for step in range(ITERS):
+        for group in ORDER:
+            plan.append(local_jobs(group, range(degree)))
+        for index, group in enumerate(ORDER):
+            plan.append(halo_jobs(index))
+            if step + 1 < ITERS:
+                plan.append(select_jobs(group))
     units = Units(join(*plan))
-    per_entry = local // TILE
-    units.run(AHEAD * per_entry)
-    for index, (step, group) in enumerate(turns):
-        for j in range(len(OFFSETS)):
-            parcel(step, group, j).wait_recv()
-        if group == 0:
-            band_copy(step, 0).wait_recv()
-        if group == groups - 1:
-            band_copy(step, 1).wait_recv()
-        arrived = parcel_in[step, group].T[:block]
-        arrived = jnp.concatenate([arrived, jnp.zeros((block, TILE - halo), F32)], axis=1)
-        halo_parts[index % 2, 0], halo_parts[index % 2, 1] = split(arrived)
-        units.run((degree - AHEAD) * per_entry)
-        units.run(degree)
-        for unit in range(2):
-            update(step, group, unit)
-        if index + 1 < len(turns):
-            units.run(AHEAD * per_entry)
-        for unit in range(2):
-            finish(step, group, unit)
-        if step + 1 < ITERS:
+    for step in range(ITERS):
+        for group in ORDER:
+            units.run(degree * (local // TILE))
+            for unit in range(2):
+                ready[group, :, cut(unit)] = gathered(unit)
+        for group in ORDER:
+            for unit in range(2):
+                prepare(step, group, unit)
+        for index, group in enumerate(ORDER):
+            for j in range(len(OFFSETS)):
+                parcel(step, group, j).wait_recv()
+            arrived = parcel_in[step, group].T[:block]
+            arrived = jnp.concatenate([arrived, jnp.zeros((block, TILE - halo), F32)], axis=1)
+            halo_parts[index % 2, 0], halo_parts[index % 2, 1] = split(arrived)
             if group == 0:
-                band_copy(step + 1, 1).start()
+                band_copy(step, 0).wait_recv()
             if group == groups - 1:
-                band_copy(step + 1, 0).start()
-            units.run(1)
-            send_group(step + 1, group)
+                band_copy(step, 1).wait_recv()
+            units.run(degree)
+            for unit in range(2):
+                finish(step, group, unit)
+            if step + 1 < ITERS:
+                units.run(1)
+                send_group(step + 1, group)
+                send_bands(step + 1, group)
 
     for step in range(ITERS):
         for group in range(groups):
@@ -439,13 +487,12 @@
     trig[:, 0] = np.cos(theta)
     trig[:, 1] = np.sin(theta)
     vmem = pl.BlockSpec(memory_space=pltpu.VMEM)
-    smem = pl.BlockSpec(memory_space=pltpu.SMEM)
     anywhere = pl.BlockSpec(memory_space=pl.ANY)
     dma = pltpu.SemaphoreType.DMA
     return pl.pallas_call(
         functools.partial(kernel, node_count, freq_count),
-        out_shape=jax.ShapeDtypeStruct(action_old.shape, F32),
-        in_specs=[anywhere, anywhere, vmem, vmem, vmem, smem, vmem, smem, vmem, vmem, vmem],
+        out_shape=pltpu.VMEM(action_old.shape, F32),
+        in_specs=[anywhere] * 11,
         out_specs=vmem,
         scratch_shapes=[
             pltpu.VMEM((bands, angles, local), F32),
@@ -461,11 +508,21 @@
             pltpu.VMEM((local, TILE), BF16),
             pltpu.VMEM((groups, 2, block, local), BF16),
             pltpu.VMEM((2, 2, block, TILE), BF16),
-            pltpu.VMEM((block, local), F32),
+            pltpu.VMEM((groups, block, local), F32),
             pltpu.VMEM((ITERS, groups, halo, 128), F32),
             pltpu.VMEM((ITERS, groups, halo, 128), F32),
             pltpu.VMEM((ITERS, 2, edge, local), F32),
-            dma((2,)),
+            pltpu.VMEM((1, local), F32),
+            pltpu.VMEM((1, local), F32),
+            pltpu.VMEM((1, local), F32),
+            pltpu.SMEM((1, bands), F32),
+            pltpu.VMEM((2, degree, local), F32),
+            pltpu.SMEM((1, slots), jnp.int32),
+            pltpu.VMEM((slots, 1, width), jnp.int32),
+            pltpu.VMEM((degree, local), jnp.int32),
+            pltpu.VMEM((2 * angles, 128), F32),
+            dma((10,)),
+            dma((bands,)),
             dma((ITERS, groups, slots)),
             dma((ITERS, groups, slots)),
             dma((ITERS, 2)),

time: 40.6 us -> 34 us (0.84)
  Pallas kernels: 38.3 us -> 33.1 us
  local copies, waits for them, and re-layouts: 2.03 us -> 0.87 us
    pallas_call x1, Pallas kernels: 38.3 us -> 33.1 us  [body(): pl.pallas_call(functools.partial(kernel, node_count, freq_count), out_sha...]
    unnamed x1, local copies, waits for them, and re-layouts: 2.03 us -> 0.87 us
where the time goes in v2:
time: 34 us
  Pallas kernels  33.1 us (97%)
  local copies, waits for them, and re-layouts  0.87 us (3%)
    pallas_call x1, Pallas kernels, body(): pl.pallas_call(functools.partial(kernel, node_count, freq_count), out_sha...  33.1 us
    unnamed x1, local copies, waits for them, and re-layouts  0.87 us

profile of v2, /device:TPU:1, one launch (start us, length us, event | category | flops | bytes accessed | tf_op | source)
XLA Modules:
  0.0 34.0 jit_solution(1955212991953537388)
XLA Ops:
  0.0 33.1 %shard_map.109 = f32[9,36,512]{2,1,0:T(8,128)S(1)} custom-call(f32[9,36,512]{2,1,0:T(8,128)} %refs_0_.1, f32[9,36,512]{2,1,0:T(8,128)} %refs_1_.1, f32[1,512]{1,0:T(1,128)} %bitcast.6, f32[1,512]{1,0:T(1,128)} %bitcast.7, f32[1,512]{1,0:T(1,128)} %bitcast.8, f32[1,9]{1,0:T(1,128)} %bitcast.9, f32[2,8,512]{2,1,0:T(8,128)} %refs_6_.1, s32[1,6]{1,0:T(1,128)} %refs_7_.1, ...), custom_call_target="tpu_custom_call" | custom-call | tf_op jit(solution)/shard_map/pallas_call | solution.py:492
  33.1 0.9 %copy.13 = f32[9,36,512]{2,1,0:T(8,128)} copy(f32[9,36,512]{2,1,0:T(8,128)S(1)} %shard_map.109) | data formatting | bytes 1327104

commit v3 on v2

--- a/solution.py
+++ b/solution.py
@@ -18,6 +18,7 @@
 STRIDE = 3
 ORDER = (0, 2, 1)
 TILE = 256
+FILL = 4
 VMEM_LIMIT = 66100000
 
 
@@ -105,10 +106,8 @@
     adjacency_ref,
     trig_ref,
     load_sem,
-    old_sem,
     send_sem,
     recv_sem,
-    band_send_sem,
     band_recv_sem,
 ):
     bands, angles, local = old_in.shape
@@ -127,12 +126,10 @@
     def band_at(offset):
         return lax.rem(band_me + offset + freq_count, freq_count)
 
-    def old_load(f):
-        return pltpu.make_async_copy(old_hbm.at[f], old_in.at[f], old_sem.at[f])
-
     pairs = (
         (nbr_hbm, nbr_ref),
         (send_hbm, send_ref),
+        (old_hbm, old_in),
         (adjacency_hbm, adjacency_ref),
         (normals_hbm, normals_ref),
         (trig_hbm, trig_ref),
@@ -143,12 +140,7 @@
         (source_hbm, source_in),
     )
     loads = [pltpu.make_async_copy(*pair, load_sem.at[i]) for i, pair in enumerate(pairs)]
-    for load in loads[:2]:
-        load.start()
-    for group in ORDER:
-        for i in range(members):
-            old_load(group + i * STRIDE).start()
-    for load in loads[2:]:
+    for load in loads:
         load.start()
     barrier = pltpu.get_barrier_semaphore()
     for offset in OFFSETS:
@@ -165,9 +157,39 @@
         return pltpu.make_async_remote_copy(
             src_ref=parcel_out.at[step, group, piece],
             dst_ref=parcel_in.at[step, group, piece],
-            send_sem=send_sem.at[step, group, j],
-            recv_sem=recv_sem.at[step, group, j],
+            send_sem=send_sem.at[0],
+            recv_sem=recv_sem.at[step, group],
             device_id={"node": node_at(OFFSETS[j])},
+            device_id_type=MESH,
+        )
+
+    def group_parcels(step, group):
+        return pltpu.make_async_remote_copy(
+            src_ref=parcel_out.at[step, group],
+            dst_ref=parcel_in.at[step, group],
+            send_sem=send_sem.at[0],
+            recv_sem=recv_sem.at[step, group],
+            device_id={"node": node_at(OFFSETS[0])},
+            device_id_type=MESH,
+        )
+
+    def all_parcels():
+        return pltpu.make_async_remote_copy(
+            src_ref=parcel_out,
+            dst_ref=parcel_in,
+            send_sem=send_sem.at[0],
+            recv_sem=recv_sem.at[0, 0],
+            device_id={"node": node_at(OFFSETS[0])},
+            device_id_type=MESH,
+        )
+
+    def all_bands():
+        return pltpu.make_async_remote_copy(
+            src_ref=band_in,
+            dst_ref=band_in,
+            send_sem=send_sem.at[1],
+            recv_sem=band_recv_sem.at[0, 0],
+            device_id={"freq": band_at(1)},
             device_id_type=MESH,
         )
 
@@ -176,7 +198,7 @@
         return pltpu.make_async_remote_copy(
             src_ref=spectra.at[step, (groups - 1, 0)[side], pl.ds(row, edge)],
             dst_ref=band_in.at[step, side],
-            send_sem=band_send_sem.at[step, side],
+            send_sem=send_sem.at[1],
             recv_sem=band_recv_sem.at[step, side],
             device_id={"freq": band_at((1, -1)[side])},
             device_id_type=MESH,
@@ -247,12 +269,12 @@
         if group == groups - 1:
             band_copy(step, 0).start()
 
+    for load in loads[:2]:
+        load.wait()
     for unit in range(2):
         for total in totals[unit]:
             pltpu.matmul_pop(total)
 
-    for load in loads[:2]:
-        load.wait()
     chosen = []
     for offset in OFFSETS:
         target = node_at(offset)
@@ -270,19 +292,7 @@
         fill = jnp.zeros((block - members * angles, local), F32)
         return jnp.concatenate(rows + [fill], axis=0)
 
-    units = Units(join(*[select_jobs(group) for group in ORDER]))
-    pl.semaphore_wait(barrier, len(OFFSETS) + 2)
-    for group in ORDER:
-        for i in range(members):
-            old_load(group + i * STRIDE).wait()
-        value = pack(old_in, group)
-        spectra[0, group] = value
-        parts[group, 0], parts[group, 1] = split(value)
-        units.run(1)
-        send_group(0, group)
-        send_bands(0, group)
-
-    for load in loads[2:-1]:
+    for load in loads[3:-1]:
         load.wait()
     adjacency = adjacency_ref[...]
     own = lax.broadcasted_iota(jnp.int32, adjacency.shape, 1)
@@ -335,6 +345,17 @@
     fixed = time_weight + jnp.abs(turning) + jnp.abs(freq_shift)
     outward = jnp.concatenate([outward, outward[: block - period]], axis=0)
     fixed = jnp.concatenate([fixed, fixed[: block - period]], axis=0)
+    units = Units(join(*[select_jobs(group) for group in ORDER]))
+    pl.semaphore_wait(barrier, len(OFFSETS) + 2)
+    loads[2].wait()
+    for group in ORDER:
+        value = pack(old_in, group)
+        spectra[0, group] = value
+        parts[group, 0], parts[group, 1] = split(value)
+        units.run(1)
+        send_group(0, group)
+        send_bands(0, group)
+
     loads[-1].wait()
     row_ids = lax.broadcasted_iota(jnp.int32, (block, local), 0)
     for group in ORDER:
@@ -386,9 +407,7 @@
         inflow = turn[0, :, columns] * before + turn[1, :, columns] * after
         inflow = inflow + rising[:, unit * TILE : (unit + 1) * TILE] * below
         inflow = inflow + falling[:, unit * TILE : (unit + 1) * TILE] * above
-        value = base[group, :, columns] + inflow * inverse[group, :, columns]
-        value = value + speed_inverse[group, :, columns] * ready[group, :, columns]
-        ready[group, :, columns] = value
+        ready[group, :, columns] = base[group, :, columns] + inflow * inverse[group, :, columns]
 
     def finish(step, group, unit):
         columns = cut(unit)
@@ -417,47 +436,60 @@
             parts[group, 0, :, columns] = high
             parts[group, 1, :, columns] = low
 
-    plan = []
+    def arrive(step, index):
+        group = ORDER[index]
+        group_parcels(step, group).wait_recv()
+        arrived = parcel_in[step, group].T[:block]
+        arrived = jnp.concatenate([arrived, jnp.zeros((block, TILE - halo), F32)], axis=1)
+        halo_parts[index % 2, 0], halo_parts[index % 2, 1] = split(arrived)
+        if group == 0:
+            band_copy(step, 0).wait_recv()
+        if group == groups - 1:
+            band_copy(step, 1).wait_recv()
+
+    first = ORDER[0]
+    plan = [local_jobs(first, range(FILL))]
     for step in range(ITERS):
-        for group in ORDER:
+        plan.append(local_jobs(first, range(FILL, degree)))
+        for group in ORDER[1:]:
             plan.append(local_jobs(group, range(degree)))
         for index, group in enumerate(ORDER):
             plan.append(halo_jobs(index))
             if step + 1 < ITERS:
+                if index + 1 == len(ORDER):
+                    plan.append(local_jobs(first, range(FILL)))
                 plan.append(select_jobs(group))
     units = Units(join(*plan))
+    per_entry = local // TILE
+    units.run(FILL * per_entry)
     for step in range(ITERS):
-        for group in ORDER:
-            units.run(degree * (local // TILE))
-            for unit in range(2):
-                ready[group, :, cut(unit)] = gathered(unit)
         for group in ORDER:
             for unit in range(2):
                 prepare(step, group, unit)
+        units.run((degree - FILL) * per_entry)
+        for group in ORDER:
+            if group != first:
+                units.run(degree * per_entry)
+            for unit in range(2):
+                columns = cut(unit)
+                local_part = speed_inverse[group, :, columns] * gathered(unit)
+                ready[group, :, columns] = ready[group, :, columns] + local_part
+        arrive(step, 0)
         for index, group in enumerate(ORDER):
-            for j in range(len(OFFSETS)):
-                parcel(step, group, j).wait_recv()
-            arrived = parcel_in[step, group].T[:block]
-            arrived = jnp.concatenate([arrived, jnp.zeros((block, TILE - halo), F32)], axis=1)
-            halo_parts[index % 2, 0], halo_parts[index % 2, 1] = split(arrived)
-            if group == 0:
-                band_copy(step, 0).wait_recv()
-            if group == groups - 1:
-                band_copy(step, 1).wait_recv()
             units.run(degree)
             for unit in range(2):
                 finish(step, group, unit)
+            if index + 1 < len(ORDER):
+                arrive(step, index + 1)
+            elif step + 1 < ITERS:
+                units.run(FILL * per_entry)
             if step + 1 < ITERS:
                 units.run(1)
                 send_group(step + 1, group)
                 send_bands(step + 1, group)
 
-    for step in range(ITERS):
-        for group in range(groups):
-            for j in range(len(OFFSETS)):
-                parcel(step, group, j).wait_send()
-        for side in range(2):
-            band_copy(step, side).wait_send()
+    all_parcels().wait_send()
+    all_bands().wait_send()
 
 
 def body(
@@ -521,11 +553,9 @@
             pltpu.VMEM((slots, 1, width), jnp.int32),
             pltpu.VMEM((degree, local), jnp.int32),
             pltpu.VMEM((2 * angles, 128), F32),
-            dma((10,)),
-            dma((bands,)),
-            dma((ITERS, groups, slots)),
-            dma((ITERS, groups, slots)),
-            dma((ITERS, 2)),
+            dma((11,)),
+            dma((2,)),
+            dma((ITERS, groups)),
             dma((ITERS, 2)),
         ],
         compiler_params=pltpu.CompilerParams(

time: 34 us -> 32.4 us (0.953)
  Pallas kernels: 33.1 us -> 31.4 us
    pallas_call x1, Pallas kernels: 33.1 us -> 31.4 us  [body(): pl.pallas_call(functools.partial(kernel, node_count, freq_count), out_sha...]
where the time goes in v3:
time: 32.4 us; the launch traced here: 32.3 us
  Pallas kernels  31.4 us (97%)
  local copies, waits for them, and re-layouts  0.87 us (3%)
    pallas_call x1, Pallas kernels, body(): pl.pallas_call(functools.partial(kernel, node_count, freq_count), out_sha...  31.4 us
    unnamed x1, local copies, waits for them, and re-layouts  0.87 us

profile of v3, /device:TPU:1, one launch (start us, length us, event | category | flops | bytes accessed | tf_op | source)
XLA Modules:
  0.0 32.3 jit_solution(9909981220884868831)
XLA Ops:
  0.0 31.4 %shard_map.109 = f32[9,36,512]{2,1,0:T(8,128)S(1)} custom-call(f32[9,36,512]{2,1,0:T(8,128)} %refs_0_.1, f32[9,36,512]{2,1,0:T(8,128)} %refs_1_.1, f32[1,512]{1,0:T(1,128)} %bitcast.6, f32[1,512]{1,0:T(1,128)} %bitcast.7, f32[1,512]{1,0:T(1,128)} %bitcast.8, f32[1,9]{1,0:T(1,128)} %bitcast.9, f32[2,8,512]{2,1,0:T(8,128)} %refs_6_.1, s32[1,6]{1,0:T(1,128)} %refs_7_.1, ...), custom_call_target="tpu_custom_call" | custom-call | tf_op jit(solution)/shard_map/pallas_call | solution.py:524
  31.5 0.9 %copy.13 = f32[9,36,512]{2,1,0:T(8,128)} copy(f32[9,36,512]{2,1,0:T(8,128)S(1)} %shard_map.109) | data formatting | bytes 1327104

commit v4 on v3

--- a/solution.py
+++ b/solution.py
@@ -321,6 +321,17 @@
         lax.fori_loop(0, out.shape[1] // chunk, fill, 0)
 
     fill_from(pick_local, adjacency)
+    units = Units(join(*[select_jobs(group) for group in ORDER]))
+    pl.semaphore_wait(barrier, len(OFFSETS) + 2)
+    loads[2].wait()
+    for group in ORDER:
+        value = pack(old_in, group)
+        spectra[0, group] = value
+        parts[group, 0], parts[group, 1] = split(value)
+        send_bands(0, group)
+        units.run(1)
+        send_group(0, group)
+
     fill_from(pick_halo, in_halo)
 
     period = 2 * angles
@@ -345,17 +356,6 @@
     fixed = time_weight + jnp.abs(turning) + jnp.abs(freq_shift)
     outward = jnp.concatenate([outward, outward[: block - period]], axis=0)
     fixed = jnp.concatenate([fixed, fixed[: block - period]], axis=0)
-    units = Units(join(*[select_jobs(group) for group in ORDER]))
-    pl.semaphore_wait(barrier, len(OFFSETS) + 2)
-    loads[2].wait()
-    for group in ORDER:
-        value = pack(old_in, group)
-        spectra[0, group] = value
-        parts[group, 0], parts[group, 1] = split(value)
-        units.run(1)
-        send_group(0, group)
-        send_bands(0, group)
-
     loads[-1].wait()
     row_ids = lax.broadcasted_iota(jnp.int32, (block, local), 0)
     for group in ORDER:
@@ -442,6 +442,8 @@
         arrived = parcel_in[step, group].T[:block]
         arrived = jnp.concatenate([arrived, jnp.zeros((block, TILE - halo), F32)], axis=1)
         halo_parts[index % 2, 0], halo_parts[index % 2, 1] = split(arrived)
+
+    def arrive_band(step, group):
         if group == 0:
             band_copy(step, 0).wait_recv()
         if group == groups - 1:
@@ -477,8 +479,11 @@
         arrive(step, 0)
         for index, group in enumerate(ORDER):
             units.run(degree)
+            arrive_band(step, group)
             for unit in range(2):
                 finish(step, group, unit)
+            if step + 1 < ITERS:
+                send_bands(step + 1, group)
             if index + 1 < len(ORDER):
                 arrive(step, index + 1)
             elif step + 1 < ITERS:
@@ -486,7 +491,6 @@
             if step + 1 < ITERS:
                 units.run(1)
                 send_group(step + 1, group)
-                send_bands(step + 1, group)
 
     all_parcels().wait_send()
     all_bands().wait_send()

time: 32.4 us -> 31.6 us (0.975)
  Pallas kernels: 31.4 us -> 30.6 us
    pallas_call x1, Pallas kernels: 31.4 us -> 30.6 us  [body(): pl.pallas_call(functools.partial(kernel, node_count, freq_count), out_sha...]
where the time goes in v4:
time: 31.6 us; the launch traced here: 31.5 us
  Pallas kernels  30.6 us (97%)
  local copies, waits for them, and re-layouts  0.87 us (3%)
    pallas_call x1, Pallas kernels, body(): pl.pallas_call(functools.partial(kernel, node_count, freq_count), out_sha...  30.6 us
    unnamed x1, local copies, waits for them, and re-layouts  0.87 us

profile of v4, /device:TPU:1, one launch (start us, length us, event | category | flops | bytes accessed | tf_op | source)
XLA Modules:
  0.0 31.5 jit_solution(8222303750028615644)
XLA Ops:
  0.0 30.6 %shard_map.109 = f32[9,36,512]{2,1,0:T(8,128)S(1)} custom-call(f32[9,36,512]{2,1,0:T(8,128)} %refs_0_.1, f32[9,36,512]{2,1,0:T(8,128)} %refs_1_.1, f32[1,512]{1,0:T(1,128)} %bitcast.6, f32[1,512]{1,0:T(1,128)} %bitcast.7, f32[1,512]{1,0:T(1,128)} %bitcast.8, f32[1,9]{1,0:T(1,128)} %bitcast.9, f32[2,8,512]{2,1,0:T(8,128)} %refs_6_.1, s32[1,6]{1,0:T(1,128)} %refs_7_.1, ...), custom_call_target="tpu_custom_call" | custom-call | tf_op jit(solution)/shard_map/pallas_call | solution.py:528
  30.6 0.9 %copy.13 = f32[9,36,512]{2,1,0:T(8,128)} copy(f32[9,36,512]{2,1,0:T(8,128)S(1)} %shard_map.109) | data formatting | bytes 1327104

commit v5 on v4

--- a/solution.py
+++ b/solution.py
@@ -324,6 +324,7 @@
     units = Units(join(*[select_jobs(group) for group in ORDER]))
     pl.semaphore_wait(barrier, len(OFFSETS) + 2)
     loads[2].wait()
+    loads[-1].wait()
     for group in ORDER:
         value = pack(old_in, group)
         spectra[0, group] = value
@@ -356,7 +357,6 @@
     fixed = time_weight + jnp.abs(turning) + jnp.abs(freq_shift)
     outward = jnp.concatenate([outward, outward[: block - period]], axis=0)
     fixed = jnp.concatenate([fixed, fixed[: block - period]], axis=0)
-    loads[-1].wait()
     row_ids = lax.broadcasted_iota(jnp.int32, (block, local), 0)
     for group in ORDER:
         speed = jnp.full((block, local), speed_ref[0, group], F32)

time: 31.6 us -> 31.6 us (level)
  no operation moved by 1% of the time
where the time goes in v5:
time: 31.6 us; the launch traced here: 31.5 us
  Pallas kernels  30.6 us (97%)
  local copies, waits for them, and re-layouts  0.87 us (3%)
    pallas_call x1, Pallas kernels, body(): pl.pallas_call(functools.partial(kernel, node_count, freq_count), out_sha...  30.6 us
    unnamed x1, local copies, waits for them, and re-layouts  0.87 us

profile of v5, /device:TPU:1, one launch (start us, length us, event | category | flops | bytes accessed | tf_op | source)
XLA Modules:
  0.0 31.5 jit_solution(9628411184693780822)
XLA Ops:
  0.0 30.6 %shard_map.109 = f32[9,36,512]{2,1,0:T(8,128)S(1)} custom-call(f32[9,36,512]{2,1,0:T(8,128)} %refs_0_.1, f32[9,36,512]{2,1,0:T(8,128)} %refs_1_.1, f32[1,512]{1,0:T(1,128)} %bitcast.6, f32[1,512]{1,0:T(1,128)} %bitcast.7, f32[1,512]{1,0:T(1,128)} %bitcast.8, f32[1,9]{1,0:T(1,128)} %bitcast.9, f32[2,8,512]{2,1,0:T(8,128)} %refs_6_.1, s32[1,6]{1,0:T(1,128)} %refs_7_.1, ...), custom_call_target="tpu_custom_call" | custom-call | tf_op jit(solution)/shard_map/pallas_call | solution.py:528
  30.6 0.9 %copy.13 = f32[9,36,512]{2,1,0:T(8,128)} copy(f32[9,36,512]{2,1,0:T(8,128)S(1)} %shard_map.109) | data formatting | bytes 1327104

commit v6 on v5

--- a/solution.py
+++ b/solution.py
@@ -256,12 +256,18 @@
     def join(*lists):
         return [[job for jobs in lists for job in jobs[unit]] for unit in range(2)]
 
-    def send_group(step, group):
+    def pick_group(step, group):
         picked = pltpu.matmul_pop(totals[0][degree]) + pltpu.matmul_pop(totals[1][degree])
         picked = jnp.concatenate([picked, jnp.zeros((128 - block, TILE), F32)], axis=0)
         parcel_out[step, group] = picked.T[:halo]
+
+    def start_group(step, group):
         for j in reversed(range(len(OFFSETS))):
             parcel(step, group, j).start()
+
+    def send_group(step, group):
+        pick_group(step, group)
+        start_group(step, group)
 
     def send_bands(step, group):
         if group == 0:
@@ -322,16 +328,18 @@
 
     fill_from(pick_local, adjacency)
     units = Units(join(*[select_jobs(group) for group in ORDER]))
-    pl.semaphore_wait(barrier, len(OFFSETS) + 2)
     loads[2].wait()
     loads[-1].wait()
     for group in ORDER:
         value = pack(old_in, group)
         spectra[0, group] = value
         parts[group, 0], parts[group, 1] = split(value)
+        units.run(1)
+        pick_group(0, group)
+        if group == ORDER[0]:
+            pl.semaphore_wait(barrier, len(OFFSETS) + 2)
         send_bands(0, group)
-        units.run(1)
-        send_group(0, group)
+        start_group(0, group)
 
     fill_from(pick_halo, in_halo)
 

time: 31.6 us -> 31.2 us (0.987)
    pallas_call x1, Pallas kernels: 30.6 us -> 30.3 us  [body(): pl.pallas_call(functools.partial(kernel, node_count, freq_count), out_sha...]
where the time goes in v6:
time: 31.2 us; the launch traced here: 31.1 us
  Pallas kernels  30.3 us (97%)
  local copies, waits for them, and re-layouts  0.87 us (3%)
    pallas_call x1, Pallas kernels, body(): pl.pallas_call(functools.partial(kernel, node_count, freq_count), out_sha...  30.3 us
    unnamed x1, local copies, waits for them, and re-layouts  0.87 us

profile of v6, /device:TPU:1, one launch (start us, length us, event | category | flops | bytes accessed | tf_op | source)
XLA Modules:
  0.0 31.1 jit_solution(6893905112149551414)
XLA Ops:
  0.0 30.3 %shard_map.109 = f32[9,36,512]{2,1,0:T(8,128)S(1)} custom-call(f32[9,36,512]{2,1,0:T(8,128)} %refs_0_.1, f32[9,36,512]{2,1,0:T(8,128)} %refs_1_.1, f32[1,512]{1,0:T(1,128)} %bitcast.6, f32[1,512]{1,0:T(1,128)} %bitcast.7, f32[1,512]{1,0:T(1,128)} %bitcast.8, f32[1,9]{1,0:T(1,128)} %bitcast.9, f32[2,8,512]{2,1,0:T(8,128)} %refs_6_.1, s32[1,6]{1,0:T(1,128)} %refs_7_.1, ...), custom_call_target="tpu_custom_call" | custom-call | tf_op jit(solution)/shard_map/pallas_call | solution.py:536
  30.3 0.9 %copy.13 = f32[9,36,512]{2,1,0:T(8,128)} copy(f32[9,36,512]{2,1,0:T(8,128)S(1)} %shard_map.109) | data formatting | bytes 1327104
